TPU v7x, 128 devices: a whole 4x4x4 slice. The times are simulated.
128 devices in a mesh: seq: 8 (over y, core), span: 16 (over x, z).
Axes of the slice: x: 4, y: 4, z: 4, core: 2. Of those that a mesh axis runs over, the one named last changes fastest.
Arguments:
- queries: bfloat16 [16, 1024, 1536], P('span', 'seq'), may hold values from -6 to 6
- key_head_matrix: bfloat16 [16, 1024, 512], P('span', 'seq'), may hold values from -6 to 6
- value_head_matrix: bfloat16 [16, 1024, 512], P('span', 'seq'), may hold values from -6 to 6
- attn_output: bfloat16 [16, 1024, 1536], P('span', 'seq'), may hold values from -6 to 6
- out_grad: bfloat16 [16, 1024, 1536], P('span', 'seq'), may hold values from -6 to 6
Outputs:
- query_grad: bfloat16 [16, 1024, 1536], P('span', 'seq')
- key_grad: bfloat16 [16, 1024, 512], P('span', 'seq')
- value_grad: bfloat16 [16, 1024, 512], P('span', 'seq')
All inputs are finite; a program needn't handle non-finite values.
Results may differ from a plain program's by a relative error of at most 0.005.
Values may be sent and summed in bfloat16 or wider, within the bound.
A program may use at most 64 MiB of HBM per device.

v0:
```python
import math
import jax
import jax.numpy as jnp
from jax import lax
from jax.sharding import PartitionSpec as P

HEAD_WIDTH = 64
QUERY_PER_KEY = 3
NEG_LARGE = -1e30


def sent_together(arrays, axis, dim, along):
    ends, at = ([], 0)
    for a in arrays[:-1]:
        at += a.shape[along]
        ends.append(at)
    both = jnp.concatenate(arrays, axis=along)
    return tuple(
        jnp.split(lax.psum_scatter(both, axis, scatter_dimension=dim, tiled=True), ends, axis=along)
    )


def spread_rows(source, seq_count):
    return source.reshape(source.shape[1], seq_count, source.shape[2] // seq_count)


def over_blocks(update, running, arrays, offset, block_rows, live_test):
    row_total = arrays[0].shape[0]
    block_total = row_total // block_rows

    def visit(block_number, running_state):
        first_row = block_number * block_rows
        slices = tuple(
            (lax.dynamic_slice_in_dim(member, first_row, block_rows, 0) for member in arrays)
        )
        position = offset + first_row
        return lax.cond(
            live_test(position),
            lambda current: update(current, slices, position),
            lambda current: current,
            running_state,
        )

    return lax.fori_loop(0, block_total, visit, running)


def per_device(queries, key_head_matrix, value_head_matrix, attn_output, out_grad):
    seq_count = lax.axis_size("seq")
    own_block = lax.axis_index("span")
    tok_local = queries.shape[1]
    kv_local = key_head_matrix.shape[2] // (HEAD_WIDTH * seq_count)
    block_len = tok_local * seq_count
    scaling = 1.0 / math.sqrt(HEAD_WIDTH)
    exchanged = (
        lax.all_to_all(
            spread_rows(queries, seq_count), "seq", split_axis=1, concat_axis=0, tiled=True
        ),
        lax.all_to_all(
            spread_rows(out_grad, seq_count), "seq", split_axis=1, concat_axis=0, tiled=True
        ),
        lax.all_to_all(
            spread_rows(attn_output, seq_count), "seq", split_axis=1, concat_axis=0, tiled=True
        ),
        lax.all_to_all(
            spread_rows(key_head_matrix, seq_count), "seq", split_axis=1, concat_axis=0, tiled=True
        ),
        lax.all_to_all(
            spread_rows(value_head_matrix, seq_count),
            "seq",
            split_axis=1,
            concat_axis=0,
            tiled=True,
        ),
    )
    query_flat = exchanged[0].reshape(block_len, kv_local * QUERY_PER_KEY * HEAD_WIDTH)
    grad_flat = exchanged[1].reshape(block_len, kv_local * QUERY_PER_KEY * HEAD_WIDTH)
    query_split = query_flat.reshape(block_len, kv_local, QUERY_PER_KEY, HEAD_WIDTH)
    grad_split = grad_flat.reshape(block_len, kv_local, QUERY_PER_KEY, HEAD_WIDTH)
    output_split = exchanged[2].reshape(block_len, kv_local, QUERY_PER_KEY, HEAD_WIDTH)
    key_flat = exchanged[3].reshape(block_len, kv_local * HEAD_WIDTH)
    value_flat = exchanged[4].reshape(block_len, kv_local * HEAD_WIDTH)
    row_delta = jnp.transpose(
        jnp.sum(grad_split.astype(jnp.float32) * output_split.astype(jnp.float32), axis=3),
        (1, 2, 0),
    )
    own_first = own_block * block_len
    query_pos = own_first + lax.iota(jnp.int32, block_len)

    def key_live(position):
        return position < own_first + block_len

    def key_scores(key_block, position):
        rows_here = key_block.shape[0]
        key_split = key_block.reshape(rows_here, kv_local, HEAD_WIDTH)
        scores = (
            jnp.einsum("tgjd,rgd->gjtr", query_split, key_split, preferred_element_type=jnp.float32)
            * scaling
        )
        key_pos = position + lax.iota(jnp.int32, rows_here)
        allowed = key_pos[None, :] <= query_pos[:, None]
        return (key_split, scores, allowed)

    def stats_update(running_state, slices, position):
        row_max, row_sum = running_state
        key_split, scores, allowed = key_scores(slices[0], position)
        masked = jnp.where(allowed, scores, NEG_LARGE)
        new_max = jnp.maximum(row_max, jnp.max(masked, axis=3))
        weights = jnp.where(allowed, jnp.exp(scores - new_max[..., None]), 0.0)
        new_sum = row_sum * jnp.exp(row_max - new_max) + jnp.sum(weights, axis=3)
        return (new_max, new_sum)

    stats_init = (
        jnp.full((kv_local, QUERY_PER_KEY, block_len), NEG_LARGE, jnp.float32),
        jnp.zeros((kv_local, QUERY_PER_KEY, block_len), jnp.float32),
    )
    key_whole, value_whole = (
        lax.all_gather(key_flat, "span", axis=0, tiled=True),
        lax.all_gather(value_flat, "span", axis=0, tiled=True),
    )
    row_max, row_sum = over_blocks(stats_update, stats_init, (key_whole,), 0, block_len, key_live)
    log_norm = row_max + jnp.log(row_sum)

    def key_side(slices, position):
        key_split, scores, allowed = key_scores(slices[0], position)
        value_split = slices[1].reshape(slices[1].shape[0], kv_local, HEAD_WIDTH)
        prob_weights = jnp.where(allowed, jnp.exp(scores - log_norm[..., None]), 0.0)
        prob_grad = jnp.einsum(
            "tgjd,rgd->gjtr", grad_split, value_split, preferred_element_type=jnp.float32
        )
        score_low = (prob_weights * (prob_grad - row_delta[..., None])).astype(jnp.bfloat16)
        query_term = scaling * jnp.einsum(
            "gjtr,rgd->tgjd", score_low, key_split, preferred_element_type=jnp.float32
        )
        return (prob_weights, score_low, query_term)

    def partial_update(running_state, slices, position):
        query_acc, key_acc, value_acc = running_state
        prob_weights, score_low, query_term = key_side(slices, position)
        rows_here = slices[0].shape[0]
        key_term = scaling * jnp.einsum(
            "gjtr,tgjd->rgd", score_low, query_split, preferred_element_type=jnp.float32
        )
        value_term = jnp.einsum(
            "gjtr,tgjd->rgd",
            prob_weights.astype(jnp.bfloat16),
            grad_split,
            preferred_element_type=jnp.float32,
        )
        key_acc = lax.dynamic_update_slice_in_dim(
            key_acc, key_term.reshape(rows_here, kv_local * HEAD_WIDTH), position, 0
        )
        value_acc = lax.dynamic_update_slice_in_dim(
            value_acc, value_term.reshape(rows_here, kv_local * HEAD_WIDTH), position, 0
        )
        return (query_acc + query_term, key_acc, value_acc)

    query_zero = jnp.zeros((block_len, kv_local, QUERY_PER_KEY, HEAD_WIDTH), jnp.float32)
    buffer_zero = jnp.zeros((lax.axis_size("span") * block_len, kv_local * HEAD_WIDTH), jnp.float32)
    grad_init = (query_zero, buffer_zero, buffer_zero)
    grad_result = over_blocks(
        partial_update, grad_init, (key_whole, value_whole), 0, block_len, key_live
    )
    query_acc, key_acc, value_acc = grad_result
    key_total, value_total = sent_together((key_acc, value_acc), "span", 0, 1)
    query_out = query_acc.astype(jnp.bfloat16).reshape(
        seq_count, tok_local, kv_local * QUERY_PER_KEY * HEAD_WIDTH
    )
    key_result = key_total.astype(jnp.bfloat16).reshape(seq_count, tok_local, kv_local * HEAD_WIDTH)
    value_result = value_total.astype(jnp.bfloat16).reshape(
        seq_count, tok_local, kv_local * HEAD_WIDTH
    )
    returned = (
        lax.all_to_all(query_out, "seq", split_axis=0, concat_axis=2, tiled=True),
        lax.all_to_all(key_result, "seq", split_axis=0, concat_axis=2, tiled=True),
        lax.all_to_all(value_result, "seq", split_axis=0, concat_axis=2, tiled=True),
    )
    return (returned[0], returned[1], returned[2])


def solution(mesh):
    in_specs = (
        P("span", "seq", None),
        P("span", "seq", None),
        P("span", "seq", None),
        P("span", "seq", None),
        P("span", "seq", None),
    )
    out_specs = (P("span", "seq", None), P("span", "seq", None), P("span", "seq", None))
    return jax.shard_map(
        per_device, mesh=mesh, in_specs=in_specs, out_specs=out_specs, check_vma=False
    )
```

profile of v0, /device:TPU:1, one launch (start us, length us, event | category | flops | bytes accessed | tf_op | source)
XLA Modules:
  0.0 670.2 jit_solution(363014363874218583)
XLA Ops:
  7.2 0.0 all-gather.3.cloned.1.call-start
  7.2 1.0 copy.53
  8.2 11.0 %all_to_all.123 = bf16[128,8,64]{0,2,1:T(8,128)(2,1)S(1)} all-to-all(bf16[128,8,64]{0,2,1:T(8,128)(2,1)S(1)} %bitcast.200), channel_id=1, replica_groups=mesh['seq'=8,'span'=16] {'seq'}, dimensions={1} | all-to-all | bytes 262144 | tf_op jit(solution)/shard_map/all_to_all | solution.py:64
  19.2 0.1 copy.54
  19.3 0.7 copy.86
  20.0 0.0 all-gather.3.cloned.1.call-update
  20.0 0.0 all-gather.5.cloned.1.call-start
  20.1 1.0 copy.57
  21.1 8.5 %all_to_all.124 = bf16[128,8,64]{0,2,1:T(8,128)(2,1)S(1)} all-to-all(bf16[128,8,64]{0,2,1:T(8,128)(2,1)S(1)} %bitcast.201), channel_id=1, replica_groups=mesh['seq'=8,'span'=16] {'seq'}, dimensions={1} | all-to-all | bytes 262144 | tf_op jit(solution)/shard_map/all_to_all | solution.py:67
  29.6 0.1 copy.58
  29.7 0.7 copy.85
  30.4 0.0 all-gather.5.cloned.1.call-update
  30.4 1.9 copy.55
  32.3 4.2 all-to-all-start.1
  36.5 1.9 copy.61
  38.5 5.8 all-to-all-done.1
  44.3 4.6 all-to-all-start.4
  48.8 1.9 copy.59
  50.7 5.9 all-to-all-done.4
  56.6 4.5 all-to-all-start.3
  61.1 0.3 copy.56
  61.4 0.2 reshape_reshape.6
  61.6 0.1 convert_bitcast_fusion
  61.6 0.5 copy.62
  62.1 6.8 %all-to-all-done.3 = bf16[128,8,192]{0,2,1:T(8,128)(2,1)S(1)} async-done(((bf16[128,8,192]{0,2,1:T(8,128)(2,1)}), bf16[128,8,192]{0,2,1:T(8,128)(2,1)S(1)}, u32[]{:S(2)}, u32[]{:S(2)}) %all-to-all-start.3) | async-done | bytes 393248 | tf_op jit(solution)/shard_map/all_to_all | solution.py:58
  68.9 0.3 copy.60
  69.1 0.2 reshape_reshape.7
  69.3 0.2 fusion.49
  69.6 0.0 all-gather.3.cloned.1.call-done
  69.6 0.4 copy-done.1
  70.0 9.1 %while.38 = (s32[]{:T(128)}, f32[1,3,1024]{2,1,0:T(4,128)S(1)}, f32[1,3,1024]{2,1,0:T(4,128)S(1)}, s32[]{:T(128)}, bf16[16384,64]{0,1:T(8,128)(2,1)}, /*index=5*...) while((s32[]{:T(128)}, f32[1,3,1024]{2,1,0:T(4,128)S(1)}, ...), condition=%wide.region_5.6_spmd.clone, body=%wide.region_0.5_spmd.clone.sunk | while | flops 425730048 | bytes 33214752 | solution.py:44
  70.0 8.2 %conditional.6 = ((f32[1,3,1024]{2,1,0:T(4,128)S(1)}, f32[1,3,1024]{2,1,0:T(4,128)S(1)})) conditional(s32[]{:T(128)} %convert_element_type.97, (f32[1,3,1024]{2,1,0:T(4,128)S(1)}, f32[1,3,1024]{2,1,0:T(4,128)S(1)}) %tuple.120, (s32[]{:T(128)}, s32[]{:T(128)}, bf16[16384,64]{0,1:T(8,128)(2,1)}, bf16[1024,1,3,64]{0,3,2,1:T(8,128)(2,1)S(1)}, ...), branch_computations={%region_1.1_spmd, %region_2.4_spmd} | conditional | flops 425730048 | bytes 33210466 | solution.py:37
  70.1 0.7 broadcast_compare_fusion
  70.7 3.6 fusion.4
  74.4 3.9 fusion.7
  79.1 32.2 %all-gather.5.cloned.1.call-done = bf16[16384,64]{0,1:T(8,128)(2,1)} async-done(((bf16[1024,64]{0,1:T(8,128)(2,1)}), bf16[16384,64]{0,1:T(8,128)(2,1)}) %all-gather.5.cloned.1.call-update) | async-done | bytes 2097168 | tf_op jit(solution)/shard_map/all_gather | solution.py:118
  111.3 1.0 broadcast_in_dim.49
  112.3 2.3 broadcast_in_dim.50.clone
  114.6 2.3 broadcast_in_dim.50
  116.9 21.9 %while.39 = (s32[]{:T(128)}, f32[1024,1,3,64]{0,3,2,1:T(8,128)}, f32[16384,64]{0,1:T(8,128)}, f32[16384,64]{0,1:T(8,128)}, s32[]{:T(128)}, /*index=5*/bf16[16384...) while((s32[]{:T(128)}, f32[1024,1,3,64]{0,3,2,1:T(8,128)}, ...), condition=%wide.region_10.11_spmd.clone, body=%wide.region_7.10_spmd.clone.sunk | while | flops 2046232576 | bytes 63893872 | solution.py:44
  116.9 21.1 %conditional.7 = ((f32[1024,1,3,64]{0,3,2,1:T(8,128)}, f32[16384,64]{0,1:T(8,128)}, f32[16384,64]{0,1:T(8,128)})) conditional(s32[]{:T(128)} %convert_element_type.98, (f32[1024,1,3,64]{0,3,2,1:T(8,128)}, f32[16384,64]{0,1:T(8,128)}, f32[16384,64]{0,1:T(8,128)}) %tuple.123, (s32[]{:T(128)}, bf16[16384,64]{0,1:T(8,128)(2,1)}, s32[]{:T(128)}, ...), branch_computations={%region_8.8_spmd, %region_9.9_spmd} | conditional | flops 2046232576 | bytes 63889500 | solution.py:37
  116.9 1.6 broadcast_compare_fusion.1
  118.5 2.7 fusion.36
  121.2 5.9 fusion.19
  127.1 4.9 fusion.30
  132.0 3.3 fusion.24
  135.3 2.7 fusion.26
  138.8 7.5 %pad_maximum_fusion = f32[16384,128]{0,1:T(8,128)} fusion(f32[16384,64]{0,1:T(8,128)} %get-tuple-element.679, f32[16384,64]{0,1:T(8,128)} %get-tuple-element.678), kind=kLoop, calls=%fused_computation.56 | loop fusion | flops 2097152 | bytes 16777216 | tf_op jit(solution)/shard_map/concatenate | solution.py:17
  146.3 0.0 reduce-scatter.2.cloned.1.call-update
  146.3 1.2 convert_element_type.77
  147.5 0.1 copy.77
  147.6 0.8 copy.64
  148.4 6.5 all-to-all-start.5
  154.9 485.2 %reduce-scatter.2.cloned.1.call-done = f32[1024,128]{0,1:T(8,128)} async-done(((f32[16384,128]{0,1:T(8,128)}), f32[1024,128]{0,1:T(8,128)}) %reduce-scatter.2.cloned.1.call-update) | async-done | bytes 524304 | tf_op jit(solution)/shard_map/reduce_scatter | solution.py:19
  640.1 1.1 convert.7
  641.2 0.7 copy.87
  641.9 6.4 all-to-all-start.7
  648.3 0.7 copy.88
  648.9 4.6 all-to-all-done.7
  653.5 4.1 all-to-all-start.6
  657.6 0.9 copy.67
  658.6 0.8 copy.69
  659.3 3.6 all-to-all-done.6
  662.9 0.8 copy.68
  (76 shorter events, 0.6 us)
Async XLA Ops:
  7.2 62.4 %all-gather.3.cloned.1.call-start = ((), (), s32[]{:S(2)}) async-start(), calls=%async_computation.9 | async-start | bytes 2228224 | tf_op jit(solution)/shard_map/all_gather | solution.py:117
  20.0 91.3 %all-gather.5.cloned.1.call-start = ((), (), s32[]{:S(2)}) async-start(), calls=%async_computation.10 | async-start | bytes 2228224 | tf_op jit(solution)/shard_map/all_gather | solution.py:118
  32.3 11.9 %all-to-all-start.1 = ((bf16[128,8,192]{0,2,1:T(8,128)(2,1)}), bf16[128,8,192]{0,2,1:T(8,128)(2,1)S(1)}, u32[]{:S(2)}, u32[]{:S(2)}) async-start(bf16[128,8,192]{0,2,1:T(8,128)(2,1)} %bitcast.27), calls=%async_computation.1 | async-start | bytes 786432 | tf_op jit(solution)/shard_map/all_to_all | solution.py:55
  44.3 12.4 %all-to-all-start.4 = ((bf16[128,8,192]{0,2,1:T(8,128)(2,1)}), bf16[128,8,192]{0,2,1:T(8,128)(2,1)S(1)}, u32[]{:S(2)}, u32[]{:S(2)}) async-start(bf16[128,8,192]{0,2,1:T(8,128)(2,1)} %bitcast.36), calls=%async_computation.4 | async-start | bytes 786432 | tf_op jit(solution)/shard_map/all_to_all | solution.py:61
  56.6 12.2 %all-to-all-start.3 = ((bf16[128,8,192]{0,2,1:T(8,128)(2,1)}), bf16[128,8,192]{0,2,1:T(8,128)(2,1)S(1)}, u32[]{:S(2)}, u32[]{:S(2)}) async-start(bf16[128,8,192]{0,2,1:T(8,128)(2,1)} %bitcast.33), calls=%async_computation.3 | async-start | bytes 786432 | tf_op jit(solution)/shard_map/all_to_all | solution.py:58
  61.1 579.0 %reduce-scatter.2.cloned.1.call-start = ((), (), s32[]{:S(2)}) async-start(), calls=%async_computation.11 | async-start | bytes 8912896 | tf_op jit(solution)/shard_map/reduce_scatter | solution.py:19
  69.3 0.7 copy-start.1
  70.7 3.6 copy-start
  148.4 493.5 %all-to-all-start.5 = ((bf16[8,128,192]{1,2,0:T(8,128)(2,1)}), bf16[8,128,192]{1,2,0:T(8,128)(2,1)S(1)}, u32[]{:S(2)}, u32[]{:S(2)}) async-start(bf16[8,128,192]{1,2,0:T(8,128)(2,1)} %copy.64), calls=%async_computation.5 | async-start | bytes 786432 | tf_op jit(solution)/shard_map/all_to_all | solution.py:173
  641.9 11.6 %all-to-all-start.7 = ((bf16[8,128,64]{1,2,0:T(8,128)(2,1)}), bf16[8,128,64]{1,2,0:T(8,128)(2,1)S(1)}, u32[]{:S(2)}, u32[]{:S(2)}) async-start(bf16[8,128,64]{1,2,0:T(8,128)(2,1)} %bitcast.183), calls=%async_computation.8 | async-start | bytes 262144 | tf_op jit(solution)/shard_map/all_to_all | solution.py:175
  653.5 9.4 %all-to-all-start.6 = ((bf16[8,128,64]{1,2,0:T(8,128)(2,1)}), bf16[8,128,64]{1,2,0:T(8,128)(2,1)S(1)}, u32[]{:S(2)}, u32[]{:S(2)}) async-start(bf16[8,128,64]{1,2,0:T(8,128)(2,1)} %bitcast.184), calls=%async_computation.7 | async-start | bytes 262144 | tf_op jit(solution)/shard_map/all_to_all | solution.py:174
Sparse Core Ops, SparseCore 0:
  20.2 44.0 all-gather.2
  67.0 44.2 all-gather.4
  146.5 493.5 reduce-scatter.1
where the time goes:
time: 674 us; the launch traced here: 670 us
  waiting for transfers between devices  544 us (81%)
  starting transfers between devices  30.4 us (5%)
  matrix products  23.1 us (3%)
  local copies, waits for them, and re-layouts  21.5 us (3%)
  blocking collectives  19.5 us (3%)
  other arithmetic  16.3 us (2%)
  between operations  13.9 us (2%)
    reduce_scatter x1, waiting for transfers between devices, sent_together(): lax.psum_scatter(both, axis, scatter_dimension=dim, tiled=True)  485 us
    all_gather x1, waiting for transfers between devices, per_device(): lax.all_gather(value_flat, 'span', axis=0, tiled=True)  32.2 us
  transfers between devices with their start and end apart: 9, of which 7 were waited for; matrix products, arithmetic and copies ran while one was open for 4% of the time, Pallas kernels for 0%

commit v1 on v0

--- a/solution.py
+++ b/solution.py
@@ -113,9 +113,22 @@
         jnp.full((kv_local, QUERY_PER_KEY, block_len), NEG_LARGE, jnp.float32),
         jnp.zeros((kv_local, QUERY_PER_KEY, block_len), jnp.float32),
     )
+
+    def ranges_read(body, which_axis, along_dim):
+        everything = jnp.concatenate(
+            lax.all_to_all(
+                jnp.stack(tuple((body for _ in range(lax.axis_size(which_axis)))), 0),
+                axis_name=which_axis,
+                split_axis=0,
+                concat_axis=0,
+            ),
+            along_dim,
+        )
+        return everything
+
     key_whole, value_whole = (
         lax.all_gather(key_flat, "span", axis=0, tiled=True),
-        lax.all_gather(value_flat, "span", axis=0, tiled=True),
+        ranges_read(value_flat, "span", 0),
     )
     row_max, row_sum = over_blocks(stats_update, stats_init, (key_whole,), 0, block_len, key_live)
     log_norm = row_max + jnp.log(row_sum)

time: 674 us -> 709 us (1.052)
  waiting for transfers between devices: 544 us -> 566 us
  starting transfers between devices: 30.4 us -> 44.1 us
  blocking collectives: 19.5 us -> 11 us
    all_gather x1 -> x0, waiting for transfers between devices: 32.2 us -> none  [per_device(): lax.all_gather(value_flat, 'span', axis=0, tiled=True)]
    reduce_scatter x1, waiting for transfers between devices: 485 us -> 515 us  [sent_together(): lax.psum_scatter(both, axis, scatter_dimension=dim, tiled=True)]
    all_to_all x0 -> x2, waiting for transfers between devices: none -> 23 us  [the longest x1 19.6 us: ranges_read(): lax.all_to_all(jnp.stack(tuple((body for _ in range(lax.axis_size(which_a...]
    all_to_all x0 -> x2, starting transfers between devices: none -> 11.7 us  [the longest x1 7.6 us: ranges_read(): lax.all_to_all(jnp.stack(tuple((body for _ in range(lax.axis_size(which_a...]
    all_to_all x1 -> x0, blocking collectives: 8.49 us -> none  [per_device(): lax.all_to_all(spread_rows(value_head_matrix, seq_count), 'seq', split_ax...]
  transfers between devices with their start and end apart: 9 -> 10, of which waited for: 7 -> 8; matrix products, arithmetic and copies ran while one was open for 4% -> 3% of each run, Pallas kernels for 0% -> 0%
where the time goes in v1:
time: 709 us; the launch traced here: 705 us
  waiting for transfers between devices  566 us (80%)
  starting transfers between devices  44.1 us (6%)
  local copies, waits for them, and re-layouts  27.6 us (4%)
  matrix products  23.2 us (3%)
  other arithmetic  17.3 us (2%)
  between operations  14.2 us (2%)
  blocking collectives  11 us (2%)
    reduce_scatter x1, waiting for transfers between devices, sent_together(): lax.psum_scatter(both, axis, scatter_dimension=dim, tiled=True)  515 us
    all_to_all x1, waiting for transfers between devices, ranges_read(): lax.all_to_all(jnp.stack(tuple((body for _ in range(lax.axis_size(which_a...  19.6 us
  transfers between devices with their start and end apart: 10, of which 8 were waited for; matrix products, arithmetic and copies ran while one was open for 3% of the time, Pallas kernels for 0%

profile of v1, /device:TPU:1, one launch (start us, length us, event | category | flops | bytes accessed | tf_op | source)
XLA Modules:
  0.0 704.6 jit_solution(8619097985235125774)
XLA Ops:
  7.2 0.0 all-gather.2.cloned.1.call-start
  7.2 1.0 copy.73
  8.2 11.0 %all_to_all.128 = bf16[128,8,64]{0,2,1:T(8,128)(2,1)S(1)} all-to-all(bf16[128,8,64]{0,2,1:T(8,128)(2,1)S(1)} %bitcast.204), channel_id=1, replica_groups=mesh['seq'=8,'span'=16] {'seq'}, dimensions={1} | all-to-all | bytes 262144 | tf_op jit(solution)/shard_map/all_to_all | solution.py:64
  19.2 0.1 copy.74
  19.3 0.7 copy.108
  20.0 0.0 all-gather.2.cloned.1.call-update
  20.0 1.7 copy.77
  21.7 4.1 all-to-all-start.2
  25.8 1.9 copy.75
  27.8 3.4 all-to-all-done.2
  31.1 4.2 all-to-all-start.1
  35.3 1.9 copy.82
  37.2 5.9 all-to-all-done.1
  43.1 4.5 all-to-all-start.5
  47.6 1.9 copy.80
  49.5 5.9 all-to-all-done.5
  55.4 4.5 all-to-all-start.4
  59.9 0.1 copy.78
  60.0 7.6 %all-to-all-done.4 = bf16[128,8,192]{0,2,1:T(8,128)(2,1)S(1)} async-done(((bf16[128,8,192]{0,2,1:T(8,128)(2,1)}), bf16[128,8,192]{0,2,1:T(8,128)(2,1)S(1)}, u32[]{:S(2)}, u32[]{:S(2)}) %all-to-all-start.4) | async-done | bytes 393248 | tf_op jit(solution)/shard_map/all_to_all | solution.py:58
  67.6 1.6 stack.3
  69.2 7.6 %all-to-all-start.3 = ((bf16[16,1024,64]{1,2,0:T(8,128)(2,1)}), bf16[16,1024,64]{1,2,0:T(8,128)(2,1)S(1)}, u32[]{:S(2)}, u32[]{:S(2)}) async-start(bf16[16,1024,64]{1,2,0:T(8,128)(2,1)} %stack.3), calls=%async_computation.3 | async-start | bytes 4194304 | tf_op jit(solution)/shard_map/all_to_all | solution.py:119
  76.8 0.0 reduce-scatter.2.cloned.1.call-start
  76.9 0.3 copy.76
  77.2 0.2 reshape_reshape.6
  77.3 0.1 convert_bitcast_fusion
  77.4 0.5 copy.83
  77.9 2.0 copy.81
  79.9 1.9 reshape_reshape.7
  81.8 1.2 fusion.49
  83.0 19.6 %all-to-all-done.3 = bf16[16,1024,64]{1,2,0:T(8,128)(2,1)S(1)} async-done(((bf16[16,1024,64]{1,2,0:T(8,128)(2,1)}), bf16[16,1024,64]{1,2,0:T(8,128)(2,1)S(1)}, u32[]{:S(2)}, u32[]{:S(2)}) %all-to-all-start.3) | async-done | bytes 2097184 | tf_op jit(solution)/shard_map/all_to_all | solution.py:119
  102.6 1.5 copy.96
  104.2 9.1 %while.38 = (s32[]{:T(128)}, f32[1,3,1024]{2,1,0:T(4,128)S(1)}, f32[1,3,1024]{2,1,0:T(4,128)S(1)}, s32[]{:T(128)}, bf16[16384,64]{0,1:T(8,128)(2,1)}, /*index=5*...) while((s32[]{:T(128)}, f32[1,3,1024]{2,1,0:T(4,128)S(1)}, ...), condition=%wide.region_5.6_spmd.clone, body=%wide.region_0.5_spmd.clone.sunk | while | flops 425730048 | bytes 33214752 | solution.py:44
  104.2 8.3 %conditional.6 = ((f32[1,3,1024]{2,1,0:T(4,128)S(1)}, f32[1,3,1024]{2,1,0:T(4,128)S(1)})) conditional(s32[]{:T(128)} %convert_element_type.97, (f32[1,3,1024]{2,1,0:T(4,128)S(1)}, f32[1,3,1024]{2,1,0:T(4,128)S(1)}) %tuple.121, (s32[]{:T(128)}, s32[]{:T(128)}, bf16[16384,64]{0,1:T(8,128)(2,1)}, bf16[1024,1,3,64]{0,3,2,1:T(8,128)(2,1)S(1)}, ...), branch_computations={%region_1.1_spmd, %region_2.4_spmd} | conditional | flops 425730048 | bytes 33210466 | solution.py:37
  104.2 0.7 broadcast_compare_fusion
  104.9 3.6 fusion.4
  108.5 3.9 fusion.7
  113.3 1.0 broadcast_in_dim.49
  114.3 2.3 broadcast_in_dim.50.clone
  116.6 2.3 broadcast_in_dim.50
  118.9 22.0 %while.39 = (s32[]{:T(128)}, f32[1024,1,3,64]{0,3,2,1:T(8,128)}, f32[16384,64]{0,1:T(8,128)}, f32[16384,64]{0,1:T(8,128)}, s32[]{:T(128)}, /*index=5*/bf16[16384...) while((s32[]{:T(128)}, f32[1024,1,3,64]{0,3,2,1:T(8,128)}, ...), condition=%wide.region_10.11_spmd.clone, body=%wide.region_7.10_spmd.clone.sunk | while | flops 2046232576 | bytes 63893872 | solution.py:44
  118.9 21.2 %conditional.7 = ((f32[1024,1,3,64]{0,3,2,1:T(8,128)}, f32[16384,64]{0,1:T(8,128)}, f32[16384,64]{0,1:T(8,128)})) conditional(s32[]{:T(128)} %convert_element_type.98, (f32[1024,1,3,64]{0,3,2,1:T(8,128)}, f32[16384,64]{0,1:T(8,128)}, f32[16384,64]{0,1:T(8,128)}) %tuple.124, (s32[]{:T(128)}, bf16[16384,64]{0,1:T(8,128)(2,1)}, s32[]{:T(128)}, ...), branch_computations={%region_8.8_spmd, %region_9.9_spmd} | conditional | flops 2046232576 | bytes 63889500 | solution.py:37
  118.9 1.7 broadcast_compare_fusion.1
  120.6 2.7 fusion.36
  123.3 5.9 fusion.19
  129.2 4.9 fusion.30
  134.1 3.3 fusion.24
  137.4 2.7 fusion.26
  140.9 7.5 %pad_maximum_fusion = f32[16384,128]{0,1:T(8,128)} fusion(f32[16384,64]{0,1:T(8,128)} %get-tuple-element.679, f32[16384,64]{0,1:T(8,128)} %get-tuple-element.678), kind=kLoop, calls=%fused_computation.56 | loop fusion | flops 2097152 | bytes 16777216 | tf_op jit(solution)/shard_map/concatenate | solution.py:17
  148.4 0.0 reduce-scatter.2.cloned.1.call-update
  148.4 1.2 convert_element_type.77
  149.6 0.1 copy.99
  149.7 0.8 copy.85
  150.5 8.4 %all-to-all-start.6 = ((bf16[8,128,192]{1,2,0:T(8,128)(2,1)}), bf16[8,128,192]{1,2,0:T(8,128)(2,1)S(1)}, u32[]{:S(2)}, u32[]{:S(2)}) async-start(bf16[8,128,192]{1,2,0:T(8,128)(2,1)} %copy.85), calls=%async_computation.6 | async-start | bytes 786432 | tf_op jit(solution)/shard_map/all_to_all | solution.py:186
  159.0 515.2 %reduce-scatter.2.cloned.1.call-done = f32[1024,128]{0,1:T(8,128)} async-done(((f32[16384,128]{0,1:T(8,128)}), f32[1024,128]{0,1:T(8,128)}) %reduce-scatter.2.cloned.1.call-update) | async-done | bytes 524304 | tf_op jit(solution)/shard_map/reduce_scatter | solution.py:19
  674.1 1.1 convert.7
  675.2 0.7 copy.109
  675.9 6.5 all-to-all-start.8
  682.4 0.7 copy.110
  683.1 4.6 all-to-all-done.8
  687.6 4.1 all-to-all-start.7
  691.8 0.9 copy.88
  692.7 0.8 copy.90
  693.5 3.6 all-to-all-done.7
  697.0 0.8 copy.89
  (78 shorter events, 0.6 us)
Async XLA Ops:
  7.2 97.0 %all-gather.2.cloned.1.call-start = ((), (), s32[]{:S(2)}) async-start(), calls=%async_computation.10 | async-start | bytes 2228224 | tf_op jit(solution)/shard_map/all_gather | solution.py:130
  21.7 9.4 %all-to-all-start.2 = ((bf16[128,8,64]{0,2,1:T(8,128)(2,1)}), bf16[128,8,64]{0,2,1:T(8,128)(2,1)S(1)}, u32[]{:S(2)}, u32[]{:S(2)}) async-start(bf16[128,8,64]{0,2,1:T(8,128)(2,1)} %bitcast.30), calls=%async_computation.2 | async-start | bytes 262144 | tf_op jit(solution)/shard_map/all_to_all | solution.py:67
  31.1 12.0 %all-to-all-start.1 = ((bf16[128,8,192]{0,2,1:T(8,128)(2,1)}), bf16[128,8,192]{0,2,1:T(8,128)(2,1)S(1)}, u32[]{:S(2)}, u32[]{:S(2)}) async-start(bf16[128,8,192]{0,2,1:T(8,128)(2,1)} %bitcast.27), calls=%async_computation.1 | async-start | bytes 786432 | tf_op jit(solution)/shard_map/all_to_all | solution.py:55
  43.1 12.3 %all-to-all-start.5 = ((bf16[128,8,192]{0,2,1:T(8,128)(2,1)}), bf16[128,8,192]{0,2,1:T(8,128)(2,1)S(1)}, u32[]{:S(2)}, u32[]{:S(2)}) async-start(bf16[128,8,192]{0,2,1:T(8,128)(2,1)} %bitcast.36), calls=%async_computation.5 | async-start | bytes 786432 | tf_op jit(solution)/shard_map/all_to_all | solution.py:61
  55.4 12.2 %all-to-all-start.4 = ((bf16[128,8,192]{0,2,1:T(8,128)(2,1)}), bf16[128,8,192]{0,2,1:T(8,128)(2,1)S(1)}, u32[]{:S(2)}, u32[]{:S(2)}) async-start(bf16[128,8,192]{0,2,1:T(8,128)(2,1)} %bitcast.33), calls=%async_computation.4 | async-start | bytes 786432 | tf_op jit(solution)/shard_map/all_to_all | solution.py:58
  67.6 1.6 copy-start.1
  69.2 33.4 %all-to-all-start.3 = ((bf16[16,1024,64]{1,2,0:T(8,128)(2,1)}), bf16[16,1024,64]{1,2,0:T(8,128)(2,1)S(1)}, u32[]{:S(2)}, u32[]{:S(2)}) async-start(bf16[16,1024,64]{1,2,0:T(8,128)(2,1)} %stack.3), calls=%async_computation.3 | async-start | bytes 4194304 | tf_op jit(solution)/shard_map/all_to_all | solution.py:119
  76.8 597.3 %reduce-scatter.2.cloned.1.call-start = ((), (), s32[]{:S(2)}) async-start(), calls=%async_computation.11 | async-start | bytes 8912896 | tf_op jit(solution)/shard_map/reduce_scatter | solution.py:19
  104.9 3.6 copy-start
  150.5 525.4 %all-to-all-start.6 = ((bf16[8,128,192]{1,2,0:T(8,128)(2,1)}), bf16[8,128,192]{1,2,0:T(8,128)(2,1)S(1)}, u32[]{:S(2)}, u32[]{:S(2)}) async-start(bf16[8,128,192]{1,2,0:T(8,128)(2,1)} %copy.85), calls=%async_computation.6 | async-start | bytes 786432 | tf_op jit(solution)/shard_map/all_to_all | solution.py:186
  675.9 11.7 %all-to-all-start.8 = ((bf16[8,128,64]{1,2,0:T(8,128)(2,1)}), bf16[8,128,64]{1,2,0:T(8,128)(2,1)S(1)}, u32[]{:S(2)}, u32[]{:S(2)}) async-start(bf16[8,128,64]{1,2,0:T(8,128)(2,1)} %bitcast.185), calls=%async_computation.9 | async-start | bytes 262144 | tf_op jit(solution)/shard_map/all_to_all | solution.py:188
  687.6 9.4 %all-to-all-start.7 = ((bf16[8,128,64]{1,2,0:T(8,128)(2,1)}), bf16[8,128,64]{1,2,0:T(8,128)(2,1)S(1)}, u32[]{:S(2)}, u32[]{:S(2)}) async-start(bf16[8,128,64]{1,2,0:T(8,128)(2,1)} %bitcast.186), calls=%async_computation.8 | async-start | bytes 262144 | tf_op jit(solution)/shard_map/all_to_all | solution.py:187
Sparse Core Ops, SparseCore 0:
  20.2 44.0 all-gather.1
  148.6 525.5 reduce-scatter.1
